TPU v7x, 32 devices: a whole 2x2x4 slice. The times are simulated.
32 devices in a mesh: owner: 4 (over y, x), rows: 8 (over z, core).
Axes of the slice: x: 2, y: 2, z: 4, core: 2. Of those that a mesh axis runs over, the one named last changes fastest.
Arguments:
- train_gate: float32 [128, 2048, 768], P('owner', 'rows'), may hold values from -0.1875 to 0.1875
- other_gate: bfloat16 [128, 2048, 768], P('owner', 'rows'), may hold values from -0.0625 to 0.0625
- train_up: float32 [128, 2048, 768], P('owner', 'rows'), may hold values from -0.1875 to 0.1875
- other_up: bfloat16 [128, 2048, 768], P('owner', 'rows'), may hold values from -0.0625 to 0.0625
- router_weight: float32 [2048, 128], P('rows', 'owner'), may hold values from -0.125 to 0.125
- router_gain: float32 [2048], P('rows'), may hold values from 0.25 to 1.75
Outputs:
- ready_gate: bfloat16 [128, 2048, 768], P(('owner', 'rows'))
- ready_up: bfloat16 [128, 2048, 768], P(('owner', 'rows'))
- scale_gate: float32 [128, 768], P(('owner', 'rows'))
- scale_up: float32 [128, 768], P(('owner', 'rows'))
- serve_router: bfloat16 [2048, 128], replicated
All inputs are finite; a program needn't handle non-finite values. Where the computation divides by a largest or mean magnitude, that divisor is 1e-20 or more.
Results may differ from a plain program's by a relative error of at most 0.001.
Values may be sent and summed in bfloat16 or wider, within the bound.
A program may use at most 192 MiB of HBM per device.

v0:
```python
import jax
import jax.numpy as jnp
from jax import lax
from jax.sharding import PartitionSpec as P


def per_device(train_gate, other_gate, train_up, other_up, router_weight, router_gain):
    latest_gate = train_gate + other_gate.astype(jnp.float32)
    latest_up = train_up + other_up.astype(jnp.float32)
    scale_gate, scale_up = lax.pmax(
        (jnp.max(jnp.abs(latest_gate), axis=1), jnp.max(jnp.abs(latest_up), axis=1)), "rows"
    )
    narrow_gate, narrow_up = (
        (latest_gate / jnp.expand_dims(scale_gate, 1)).astype(jnp.bfloat16),
        (latest_up / jnp.expand_dims(scale_up, 1)).astype(jnp.bfloat16),
    )
    ready_gate, ready_up = (
        lax.all_to_all(narrow_gate, "rows", split_axis=0, concat_axis=1, tiled=True),
        lax.all_to_all(narrow_up, "rows", split_axis=0, concat_axis=1, tiled=True),
    )
    scale_gate = lax.dynamic_slice_in_dim(
        scale_gate, lax.axis_index("rows") * ready_gate.shape[0], ready_gate.shape[0], axis=0
    )
    scale_up = lax.dynamic_slice_in_dim(
        scale_up, lax.axis_index("rows") * ready_up.shape[0], ready_up.shape[0], axis=0
    )
    part_router = (router_weight * router_gain[:, None]).astype(jnp.bfloat16)
    row_router = lax.all_gather(part_router, "rows", axis=0, tiled=True)
    serve_router = lax.all_gather(row_router, "owner", axis=1, tiled=True)
    return (ready_gate, ready_up, scale_gate, scale_up, serve_router)


def solution(mesh):
    in_specs = (
        P("owner", "rows", None),
        P("owner", "rows", None),
        P("owner", "rows", None),
        P("owner", "rows", None),
        P("rows", "owner"),
        P("rows"),
    )
    out_specs = (
        P(("owner", "rows"), None, None),
        P(("owner", "rows"), None, None),
        P(("owner", "rows"), None),
        P(("owner", "rows"), None),
        P(),
    )
    return jax.shard_map(
        per_device, mesh=mesh, in_specs=in_specs, out_specs=out_specs, check_vma=False
    )
```

profile of v0, /device:TPU:17, one launch (start us, length us, event | category | flops | bytes accessed | tf_op | source)
XLA Modules:
  0.0 721.7 jit_solution(17093119717390789167)
XLA Ops:
  7.2 0.0 all-reduce.3.cloned.1.call-start
  7.2 0.0 copy-start
  7.2 0.0 copy-start.1
  7.2 14.8 %abs_reduce_fusion = f32[32,768]{1,0:T(8,128)} fusion(f32[32,256,768]{2,1,0:T(8,128)} %param.8, bf16[32,256,768]{2,1,0:T(8,128)(2,1)} %param.9), kind=kLoop, calls=%fused_computation.1 | loop fusion | flops 25141248 | bytes 37847040 | tf_op jit(solution)/shard_map/reduce_max | solution.py:11
  22.0 4.4 copy-done
  26.4 3.6 copy-done.1
  30.0 4.3 abs_reduce_fusion.1
  34.3 0.0 all-reduce.3.cloned.1.call-update
  34.3 53.4 %all-reduce.3.cloned.1.call-done = (f32[32,768]{1,0:T(8,128)}, f32[32,768]{1,0:T(8,128)}) async-done(((f32[32,768]{1,0:T(8,128)}, f32[32,768]{1,0:T(8,128)}), (f32[32,768]{1,0:T(8,128)}, f32[32,768]{1,0:T(8,128)})) %all-reduce.3.cloned.1.call-update) | async-done | bytes 196624 | tf_op jit(solution)/shard_map/pmax | solution.py:10
  87.7 29.7 %divide_convert_fusion = (bf16[32,256,768]{2,1,0:T(8,128)(2,1)}, bf16[32,256,768]{2,1,0:T(8,128)(2,1)S(1)}) fusion(f32[32,256,768]{2,1,0:T(8,128)} %param.8, bf16[32,256,768]{2,1,0:T(8,128)(2,1)} %param.9, f32[32,768]{1,0:T(8,128)} %get-tuple-element.11, f32[32,768]{1,0:T(8,128)} %get-tuple-element.10, f32[32,256,768]{2,1,0:T(8,128)} %param.6, ...), kind=kLoop, calls=%fused_computation | loop fusion | flops 50331648 | bytes 100859904 | tf_op jit(solution)/shard_map/convert_element_type | solution.py:15
  117.4 0.0 copy-start.2
  117.4 0.0 copy-start.3
  117.4 277.6 %all_to_all.36 = bf16[32,256,768]{2,1,0:T(8,128)(2,1)} all-to-all(bf16[32,256,768]{2,1,0:T(8,128)(2,1)S(1)} %get-tuple-element.13), channel_id=1, replica_groups=mesh['owner'=4,'rows'=8] {'rows'}, dimensions={0} | all-to-all | bytes 25165824 | tf_op jit(solution)/shard_map/all_to_all | solution.py:18
  395.0 9.3 %all-to-all-start.1 = ((bf16[32,256,768]{2,1,0:T(8,128)(2,1)}), bf16[32,256,768]{2,1,0:T(8,128)(2,1)}, u32[]{:S(2)}, u32[]{:S(2)}) async-start(bf16[32,256,768]{2,1,0:T(8,128)(2,1)} %get-tuple-element.12), calls=%async_computation.1 | async-start | bytes 25165824 | tf_op jit(solution)/shard_map/all_to_all | solution.py:19
  404.3 0.0 copy-done.2
  404.3 0.0 copy-done.3
  404.3 278.0 %all_gather.6 = bf16[2048,32]{0,1:T(8,128)(2,1)S(1)} all-gather(bf16[256,32]{0,1:T(8,128)(2,1)S(1)} %multiply_convert_fusion), channel_id=1, replica_groups=mesh['owner'=4,'rows'=8] {'rows'}, dimensions={0}, use_global_device_ids=true | all-gather | bytes 147456 | tf_op jit(solution)/shard_map/all_gather | solution.py:28
  682.3 8.8 %all_gather.7 = bf16[2048,128]{0,1:T(8,128)(2,1)S(1)} all-gather(bf16[2048,32]{0,1:T(8,128)(2,1)S(1)} %all_gather.6), channel_id=1, replica_groups=mesh['owner'=4,'rows'=8] {'owner'}, dimensions={1}, use_global_device_ids=true | all-gather | bytes 655360 | tf_op jit(solution)/shard_map/all_gather | solution.py:29
  691.1 1.0 copy.16
  692.1 1.4 constant_dynamic-slice_fusion
  693.4 10.7 %copy.14 = bf16[8,4,256,768]{3,2,0,1:T(8,128)(2,1)} copy(bf16[8,4,256,768]{3,2,1,0:T(8,128)(2,1)} %bitcast.8) | data formatting | bytes 25165824 | tf_op jit(solution)/shard_map/all_to_all | solution.py:18
  704.1 0.0 all-to-all-done.1
  704.1 10.7 %copy.15 = bf16[8,4,256,768]{3,2,0,1:T(8,128)(2,1)} copy(bf16[8,4,256,768]{3,2,1,0:T(8,128)(2,1)} %bitcast.3) | data formatting | bytes 25165824 | tf_op jit(solution)/shard_map/all_to_all | solution.py:19
  (1 shorter events, 0.0 us)
Async XLA Ops:
  7.2 80.6 %all-reduce.3.cloned.1.call-start = ((), (), s32[]{:S(2)}) async-start(), calls=%async_computation.2 | async-start | bytes 393216 | tf_op jit(solution)/shard_map/pmax | solution.py:10
  7.2 19.2 %copy-start = (f32[32,256,768]{2,1,0:T(8,128)S(1)}, f32[32,256,768]{2,1,0:T(8,128)}, u32[]{:S(2)}) copy-start(f32[32,256,768]{2,1,0:T(8,128)} %param.6) | copy-start | bytes 75497472
  7.2 22.8 %copy-start.1 = (bf16[32,256,768]{2,1,0:T(8,128)(2,1)S(1)}, bf16[32,256,768]{2,1,0:T(8,128)(2,1)}, u32[]{:S(2)}) copy-start(bf16[32,256,768]{2,1,0:T(8,128)(2,1)} %param.7) | copy-start | bytes 37748740
  117.4 286.8 %copy-start.2 = (f32[256,32]{0,1:T(8,128)S(1)}, f32[256,32]{0,1:T(8,128)}, u32[]{:S(2)}) copy-start(f32[256,32]{0,1:T(8,128)} %param.10) | copy-start | bytes 98308
  117.4 286.8 %copy-start.3 = (f32[256]{0:T(256)S(1)}, f32[256]{0:T(256)}, u32[]{:S(2)}) copy-start(f32[256]{0:T(256)} %param.11) | copy-start | bytes 3076
  395.0 309.1 %all-to-all-start.1 = ((bf16[32,256,768]{2,1,0:T(8,128)(2,1)}), bf16[32,256,768]{2,1,0:T(8,128)(2,1)}, u32[]{:S(2)}, u32[]{:S(2)}) async-start(bf16[32,256,768]{2,1,0:T(8,128)(2,1)} %get-tuple-element.12), calls=%async_computation.1 | async-start | bytes 25165824 | tf_op jit(solution)/shard_map/all_to_all | solution.py:19
Sparse Core Ops, SparseCore 0:
  34.5 53.2 all-reduce.2
where the time goes:
time: 727 us; the launch traced here: 722 us
  blocking collectives  564 us (78%)
  waiting for transfers between devices  53.4 us (7%)
  other arithmetic  48.8 us (7%)
  local copies, waits for them, and re-layouts  31.7 us (4%)
  between operations  14.1 us (2%)
  starting transfers between devices  9.3 us (1%)
    all_gather x1, blocking collectives, per_device(): row_router = lax.all_gather(part_router, 'rows', axis=0, tiled=True)  278 us
    all_to_all x1, blocking collectives, per_device(): lax.all_to_all(narrow_gate, 'rows', split_axis=0, concat_axis=1, tiled=True)  278 us
    pmax x1, waiting for transfers between devices, per_device(): lax.pmax((jnp.max(jnp.abs(latest_gate), axis=1), jnp.max(jnp.abs(latest_u...  53.4 us
    convert_element_type x1, other arithmetic, per_device(): (latest_up / jnp.expand_dims(scale_up, 1)).astype(jnp.bfloat16)  29.7 us
    reduce_max x1, other arithmetic, per_device(): jnp.max(jnp.abs(latest_up), axis=1)  14.8 us
  transfers between devices with their start and end apart: 2, of which 1 were waited for; matrix products, arithmetic and copies ran while one was open for 2% of the time, Pallas kernels for 0%

commit v1 on v0

v1 whole, which is shorter than its diff:
```python
import functools

import jax
import jax.numpy as jnp
from jax import lax
from jax.experimental import pallas as pl
from jax.experimental.pallas import tpu as pltpu
from jax.sharding import PartitionSpec as P

F32, BF16 = jnp.float32, jnp.bfloat16
CHUNK = 32


def flipped(me, k, n):
    out, bit = 0, 1
    while bit < n:
        out = out + ((me // bit + k // bit) % 2) * bit
        bit *= 2
    return out


def kernel(n, owners, each, train_gate, other_gate, train_up, other_up, part_router,
           ready_gate, ready_up, scales, router,
           wide, narrow, send, mx, rx, full,
           load_sem, send_sem, recv_sem, own_sem, mx_sem, rx_sem, fl_sem, fr_sem,
           rt_send, rt_recv, ro_send, ro_recv, rt_own):
    me, owner = lax.axis_index("rows"), lax.axis_index("owner")
    rows = wide.shape[2]
    units = 2 * each
    trains, others, readies = (train_gate, train_up), (other_gate, other_up), (ready_gate, ready_up)

    def loads(step):
        unit, slot = step % units, step % 2
        kind, j = unit // each, unit % each
        return (
            pltpu.make_async_copy(trains[kind].at[:, j], wide.at[slot], load_sem.at[slot, 0]),
            pltpu.make_async_copy(others[kind].at[:, j], narrow.at[slot], load_sem.at[slot, 1]),
        )

    def start(step):
        if step < 2 * units:
            for copy in loads(step):
                copy.start()

    def remote(src, dst, s, r, **where):
        return pltpu.make_async_remote_copy(
            src_ref=src, dst_ref=dst, send_sem=s, recv_sem=r, device_id=where,
            device_id_type=pl.DeviceIdType.MESH,
        )

    start(0)
    start(1)
    barrier = pltpu.get_barrier_semaphore()
    for k in range(1, n):
        pl.semaphore_signal(barrier, inc=1, device_id={"rows": (me + k) % n},
                            device_id_type=pl.DeviceIdType.MESH)
    for k in range(1, owners):
        pl.semaphore_signal(barrier, inc=1, device_id={"owner": (owner + k) % owners},
                            device_id_type=pl.DeviceIdType.MESH)
    pl.semaphore_wait(barrier, n - 1 + owners - 1)

    def router_rows(k):
        return remote(part_router, router.at[owner, me], rt_send.at[k], rt_recv.at[k],
                      rows=(me + k) % n)

    def router_owners(k):
        return remote(router.at[owner], router.at[owner], ro_send.at[k], ro_recv.at[k],
                      owner=(owner + k) % owners)

    own_router = pltpu.make_async_copy(part_router, router.at[owner, me], rt_own)
    own_router.start()
    for k in range(1, n):
        router_rows(k).start()

    for unit in range(units):
        slot = unit % 2
        for copy in loads(unit):
            copy.wait()

        def largest(d, _, slot=slot, unit=unit):
            acc = None
            for i in range(rows // CHUNK):
                x = wide[slot, d, i * CHUNK:(i + 1) * CHUNK, :]
                y = narrow[slot, d, i * CHUNK:(i + 1) * CHUNK, :].astype(F32)
                a = jnp.abs(x + y)
                acc = a if acc is None else jnp.maximum(acc, a)
            mx[d, unit:unit + 1, :] = jnp.max(acc, axis=0, keepdims=True)
            return 0

        lax.fori_loop(0, n, largest, 0)
        start(unit + 2)

    def to_owner(k):
        d = (me + k) % n
        return remote(mx.at[d], rx.at[me], mx_sem.at[k], rx_sem.at[k], rows=d)

    def to_all(k):
        return remote(scales, full.at[me], fl_sem.at[k], fr_sem.at[k], rows=(me + k) % n)

    for k in range(1, n):
        to_owner(k).start()
    rx[me] = mx[me]
    for k in range(1, n):
        to_owner(k).wait()
    total = rx[0]
    for d in range(1, n):
        total = jnp.maximum(total, rx[d])
    scales[...] = total
    full[me] = total
    for k in range(1, n):
        to_all(k).start()
    own_router.wait()
    for k in range(1, n):
        router_rows(k).wait()
    for k in range(1, owners):
        router_owners(k).start()
    for k in range(1, n):
        to_all(k).wait()

    far, near = list(range(n // 2, n)), list(range(2, n // 2))
    side = me % 2

    def dest(p):
        a, b, c = len(far), len(near), n // 2
        in_far = jnp.where(side == 0, p < a, jnp.logical_and(p >= b, p < a + b))
        at_far = p - side * b
        at_near = p - (1 - side) * a
        k = jnp.where(p == n - 2, 1, jnp.where(in_far, c + at_far, 2 + at_near))
        return flipped(me, k, n)

    def data(unit, p, d):
        kind, j = unit // each, unit % each
        return remote(send.at[unit, p], readies[kind].at[j, me], send_sem.at[unit, p],
                      recv_sem.at[unit, me], rows=d)

    def own(unit):
        kind, j = unit // each, unit % each
        return pltpu.make_async_copy(send.at[unit, n - 1], readies[kind].at[j, me], own_sem.at[unit])

    for unit in range(units):
        step = units + unit
        slot = step % 2
        for copy in loads(step):
            copy.wait()

        def scaled(p, d, slot, unit):
            inverse = 1.0 / full[d, unit:unit + 1, :]
            for i in range(rows // CHUNK):
                x = wide[slot, d, i * CHUNK:(i + 1) * CHUNK, :]
                y = narrow[slot, d, i * CHUNK:(i + 1) * CHUNK, :].astype(F32)
                send[unit, p, i * CHUNK:(i + 1) * CHUNK, :] = ((x + y) * inverse).astype(BF16)

        def one(p, _, slot=slot, unit=unit):
            d = dest(p)
            scaled(p, d, slot, unit)
            data(unit, p, d).start()
            return 0

        lax.fori_loop(0, n - 1, one, 0)
        scaled(n - 1, me, slot, unit)
        own(unit).start()
        start(step + 2)

    for unit in range(units):
        kind, j = unit // each, unit % each

        def ended(k, _, unit=unit, kind=kind, j=j):
            d = (me + k) % n
            remote(send.at[unit, k - 1], readies[kind].at[j, d], send_sem.at[unit, k - 1],
                   recv_sem.at[unit, d], rows=d).wait()
            return 0

        lax.fori_loop(1, n, ended, 0)
        own(unit).wait()
    for k in range(1, owners):
        router_owners(k).wait()


def per_device(n, owners, train_gate, other_gate, train_up, other_up, router_weight, router_gain):
    experts, rows, width = train_gate.shape
    each = experts // n
    units = 2 * each
    columns = router_weight.shape[1]
    part = (router_weight * router_gain[:, None]).astype(BF16)
    lanes = 128 if rows * columns % (128 * 16) == 0 else columns
    part = part.reshape(rows * columns // lanes, lanes)
    blocks = [x.reshape(n, each, rows, width) for x in (train_gate, other_gate, train_up, other_up)]
    hbm, vmem = pl.BlockSpec(memory_space=pl.ANY), pl.BlockSpec(memory_space=pltpu.VMEM)
    ready = jax.ShapeDtypeStruct((each, n, rows, width), BF16)
    dma = pltpu.SemaphoreType.DMA
    ready_gate, ready_up, scales, router = pl.pallas_call(
        functools.partial(kernel, n, owners, each),
        out_shape=(
            ready, ready,
            jax.ShapeDtypeStruct((units, width), F32),
            jax.ShapeDtypeStruct((owners, n) + part.shape, BF16),
        ),
        in_specs=[hbm] * 4 + [vmem],
        out_specs=(hbm, hbm, vmem, hbm),
        scratch_shapes=[
            pltpu.VMEM((2, n, rows, width), F32),
            pltpu.VMEM((2, n, rows, width), BF16),
            pltpu.VMEM((units, n, rows, width), BF16),
            pltpu.VMEM((n, units, width), F32),
            pltpu.VMEM((n, units, width), F32),
            pltpu.VMEM((n, units, width), F32),
            dma((2, 2)), dma((units, n)), dma((units, n)), dma((units,)),
            dma((n,)), dma((n,)), dma((n,)), dma((n,)),
            dma((n,)), dma((n,)), dma((owners,)), dma((owners,)), dma(()),
        ],
        compiler_params=pltpu.CompilerParams(
            collective_id=0, has_side_effects=True, vmem_limit_bytes=60 * 1024 * 1024
        ),
    )(*blocks, part)
    ready_gate, ready_up = (x.reshape(each, n * rows, width) for x in (ready_gate, ready_up))
    serve_router = (
        router.reshape(owners, n * rows, columns).transpose(1, 0, 2).reshape(n * rows, owners * columns)
    )
    return (ready_gate, ready_up, scales[:each], scales[each:], serve_router)


def solution(mesh):
    n, owners = mesh.shape["rows"], mesh.shape["owner"]
    in_specs = (
        P("owner", "rows", None),
        P("owner", "rows", None),
        P("owner", "rows", None),
        P("owner", "rows", None),
        P("rows", "owner"),
        P("rows"),
    )
    out_specs = (
        P(("owner", "rows"), None, None),
        P(("owner", "rows"), None, None),
        P(("owner", "rows"), None),
        P(("owner", "rows"), None),
        P(),
    )
    return jax.shard_map(
        functools.partial(per_device, n, owners), mesh=mesh, in_specs=in_specs,
        out_specs=out_specs, check_vma=False,
    )
```

time: 727 us -> 609 us (0.84)
  Pallas kernels: 0 us -> 580 us
  blocking collectives: 564 us -> 0 us
  waiting for transfers between devices: 53.4 us -> 0 us
  other arithmetic: 48.8 us -> 0.77 us
  between operations: 14.1 us -> 0.66 us
  starting transfers between devices: 9.3 us -> 0 us
    pallas_call x0 -> x1, Pallas kernels: none -> 580 us  [per_device(): pl.pallas_call(functools.partial(kernel, n, owners, each), out_shape=(rea...]
    all_gather x2 -> x0, blocking collectives: 287 us -> none  [the longest x1 278 us: per_device(): row_router = lax.all_gather(part_router, 'rows', axis=0, tiled=True)]
    all_to_all x1 -> x0, blocking collectives: 278 us -> none  [per_device(): lax.all_to_all(narrow_gate, 'rows', split_axis=0, concat_axis=1, tiled=True)]
    pmax x1 -> x0, waiting for transfers between devices: 53.4 us -> none  [per_device(): lax.pmax((jnp.max(jnp.abs(latest_gate), axis=1), jnp.max(jnp.abs(latest_u...]
    convert_element_type x2 -> x1, other arithmetic: 29.7 us -> 0.77 us  [per_device(): part = (router_weight * router_gain[:, None]).astype(BF16)]
    all_to_all x2 -> x0, local copies, waits for them, and re-layouts: 21.4 us -> none  [the longest x1 10.7 us: per_device(): lax.all_to_all(narrow_up, 'rows', split_axis=0, concat_axis=1, tiled=True)]
    reduce_max x2 -> x0, other arithmetic: 19.1 us -> none  [the longest x1 14.8 us: per_device(): jnp.max(jnp.abs(latest_up), axis=1)]
    unnamed x9 -> x3, local copies, waits for them, and re-layouts: 8.98 us -> 21.9 us
  transfers between devices with their start and end apart: 2 -> 0, of which waited for: 1 -> 0; matrix products, arithmetic and copies ran while one was open for 2% -> 0% of each run, Pallas kernels for 0% -> 0%
where the time goes in v1:
time: 609 us
  Pallas kernels  580 us (95%)
  local copies, waits for them, and re-layouts  27.6 us (5%)
    pallas_call x1, Pallas kernels, per_device(): pl.pallas_call(functools.partial(kernel, n, owners, each), out_shape=(rea...  580 us
    unnamed x3, local copies, waits for them, and re-layouts  21.9 us

profile of v1, /device:TPU:17, one launch (start us, length us, event | category | flops | bytes accessed | tf_op | source)
XLA Modules:
  0.0 609.0 jit_solution(8339709672399454504)
XLA Ops:
  0.6 0.8 multiply_convert_fusion
  1.4 0.1 copy.13
  1.5 0.7 reshape.42.part_router
  2.2 580.0 %shard_map.101 = (bf16[4,8,256,768]{3,2,1,0:T(8,128)(2,1)}, bf16[4,8,256,768]{3,2,1,0:T(8,128)(2,1)}, f32[8,768]{1,0:T(8,128)}, bf16[4,8,64,128]{3,2,1,0:T(8,128)(2,1)}) custom-call(f32[8,4,256,768]{3,2,1,0:T(8,128)} %bitcast.10, bf16[8,4,256,768]{3,2,1,0:T(8,128)(2,1)} %bitcast.12, f32[8,4,256,768]{3,2,1,0:T(8,128)} %bitcast.11, ...), custom_call_target="tpu_custom_call" | custom-call | tf_op jit(solution)/shard_map/pallas_call | solution.py:191
  582.3 1.4 fusion
  583.7 2.6 reshape.45
  586.3 0.8 copy.14
  587.1 1.0 copy.15
  588.1 10.4 %copy.18 = bf16[4,2048,768]{2,1,0:T(8,128)(2,1)} copy(bf16[4,2048,768]{2,1,0:T(8,128)(2,1)} %bitcast.15) | data formatting | bytes 25165824
  598.6 10.4 %copy.19 = bf16[4,2048,768]{2,1,0:T(8,128)(2,1)} copy(bf16[4,2048,768]{2,1,0:T(8,128)(2,1)} %bitcast.14) | data formatting | bytes 25165824
